TPU v7x, 512 devices: a whole 4x8x8 slice. The times are simulated.
512 devices in a mesh: group: 2 (over core), dp: 64 (over y, x, z_hi), mp: 4 (over z_lo).
Axes of the slice: x: 4, y: 8, z: 8 (z_hi: 2, z_lo: 4; z = z_hi * 4 + z_lo), core: 2. Of those that a mesh axis runs over, the one named last changes fastest.
Arguments:
- x_arrive: bfloat16 [256, 256, 1152], P(('group', 'dp')), may hold values from -6 to 6
- cond_first: int32 [128], P(('group', 'dp')), may hold values 0 or 1
- labels: int32 [128], P(('group', 'dp')), may hold values from 0 to 999
- step_ids: int32 [128], P(('group', 'dp')), may hold values from 0 to 999
- guidance: float32 [1], replicated, may hold values from 2 to 6
- time_table: bfloat16 [1000, 1152], P(None, 'mp'), may hold values from -6 to 6
- class_table: bfloat16 [1001, 1152], P(None, 'mp'), may hold values from -6 to 6
- ada_weight: bfloat16 [1152, 6912], P('mp', 'dp'), may hold values from -0.1875 to 0.1875
- final_ada: bfloat16 [1152, 2304], P('mp'), may hold values from -0.1875 to 0.1875
- qkv_weight: bfloat16 [3, 1152, 1152], P(None, 'dp', 'mp'), may hold values from -2 to 2
- proj_weight: bfloat16 [1152, 1152], P('mp', 'dp'), may hold values from -0.1875 to 0.1875
- fc1_weight: bfloat16 [1152, 4608], P('dp', 'mp'), may hold values from -0.1875 to 0.1875
- fc2_weight: bfloat16 [4608, 1152], P('mp', 'dp'), may hold values from -0.09375 to 0.09375
- out_weight: bfloat16 [1152, 16], replicated, may hold values from -0.1875 to 0.1875
Outputs:
- guided: float32 [128, 4096], P(('group', 'dp'), 'mp')
All inputs are finite; a program needn't handle non-finite values. No bound on the sum of `cond_first` on one device may be relied on, other than what follows from the above.
Results may differ from a plain program's by a relative error of at most 0.025.
Values may be sent and summed in bfloat16 or wider, within the bound.
No kernel may reach another device: no remote copies, remote signals or barrier semaphores. Data moves between devices by JAX's collectives and lax.ppermute only.
A program may use at most 64 MiB of HBM per device.

v0:
```python
import jax
import jax.numpy as jnp
from jax import lax
from jax.sharding import Mesh
from jax.sharding import PartitionSpec as P

HEADS = 16
CLASSES = 1000
DP = ("dp_0", "dp_1", "dp_2")
GROUP_DP = ("group", "dp_0", "dp_1", "dp_2")


def from_everyone(x, axis):
    size = lax.axis_size(axis)
    return lax.all_to_all(jnp.broadcast_to(x[None], (size, *x.shape)), axis, 0, 0, tiled=True)


def laid_out(pieces, dim):
    pieces = jnp.moveaxis(pieces, 0, dim)
    shape = pieces.shape
    return pieces.reshape(*shape[:dim], shape[dim] * shape[dim + 1], *shape[dim + 2 :])


def collect(x, axis, dim):
    pieces = from_everyone(x, axis)
    return laid_out(pieces, dim)


def of_everyone(x, axis):
    everything = from_everyone(x, axis)
    return jnp.sum(everything.astype(jnp.float32), axis=0)


def gathered_by_axis(x, axes, dim):
    for axis in reversed(axes):
        x = lax.all_gather(x, axis, axis=dim, tiled=True)
    return x


def cut_along(x, dim, size):
    shape = x.shape
    pieces = x.reshape(*shape[:dim], size, shape[dim] // size, *shape[dim + 1 :])
    return jnp.moveaxis(pieces, dim, 0)


def sum_at_owner(x, axis, dim):
    size = lax.axis_size(axis)
    pieces = lax.all_to_all(cut_along(x, dim, size), axis, 0, 0, tiled=True)
    return jnp.sum(pieces.astype(jnp.float32), axis=0)


def layer_norm(values):
    mean = jnp.mean(values, axis=-1, keepdims=True)
    centred = values - mean
    spread = jnp.mean(centred * centred, axis=-1, keepdims=True)
    return centred * lax.rsqrt(spread + 1e-06)


def on_device(
    x_arrive,
    cond_first,
    labels,
    step_ids,
    guidance,
    time_table,
    class_table,
    ada_weight,
    final_ada,
    qkv_weight,
    proj_weight,
    fc1_weight,
    fc2_weight,
    out_weight,
):
    pair_count = labels.shape[0]
    tokens = x_arrive.shape[1]
    width = x_arrive.shape[2]
    image_count = 2 * pair_count
    row_count = image_count * tokens
    split_rows = x_arrive.reshape(pair_count, 2, tokens, width)
    first = (cond_first == 1)[:, None, None]
    cond_rows = jnp.where(first, split_rows[:, 0], split_rows[:, 1])
    uncond_rows = jnp.where(first, split_rows[:, 1], split_rows[:, 0])
    x_sides = jnp.stack([cond_rows, uncond_rows])
    time_part = jnp.take(time_table, step_ids, axis=0).astype(jnp.float32)
    class_part = jnp.take(class_table, labels, axis=0).astype(jnp.float32)
    null_part = class_table[CLASSES].astype(jnp.float32)[None, :]
    emb_sides = time_part[None] + jnp.stack([class_part, null_part])
    act_sides = jax.nn.silu(emb_sides).astype(jnp.bfloat16)
    images, acts = (x_sides, act_sides)
    images = images.reshape(image_count, tokens, width)
    acts = acts.reshape(image_count, act_sides.shape[2])
    partial_final = jnp.dot(acts, final_ada, preferred_element_type=jnp.float32)
    every_act = collect(acts, DP, 0)
    column_part = jnp.dot(every_act, ada_weight, preferred_element_type=jnp.float32)
    summed, fmods = (
        of_everyone(column_part.astype(jnp.bfloat16), "mp").astype(jnp.float32),
        of_everyone(partial_final.astype(jnp.bfloat16), "mp").astype(jnp.float32),
    )
    mods = lax.all_to_all(
        summed.astype(jnp.bfloat16), DP, split_axis=0, concat_axis=1, tiled=True
    ).astype(summed.dtype)
    shift_a, scale_a, gate_a, shift_m, scale_m, gate_m = jnp.split(mods, 6, axis=1)
    shift_f, scale_f = jnp.split(fmods, 2, axis=1)
    images_f = images.astype(jnp.float32)
    hidden = (layer_norm(images_f) * (1.0 + scale_a[:, None]) + shift_a[:, None]).astype(
        jnp.bfloat16
    )
    hidden = hidden.reshape(row_count, width)
    quarter = qkv_weight.shape[2]
    head_dim = width // HEADS
    local_heads = quarter // head_dim
    columns = hidden
    qkv = jnp.einsum(
        "rd,kdc->krc",
        columns,
        lax.all_gather(qkv_weight, DP, axis=1, tiled=True),
        preferred_element_type=jnp.float32,
    ).astype(jnp.bfloat16)
    query = qkv[0].reshape(image_count, tokens, local_heads, head_dim)
    keys = qkv[1].reshape(image_count, tokens, local_heads, head_dim)
    values = qkv[2].reshape(image_count, tokens, local_heads, head_dim)
    scores = jnp.einsum(
        "bqhe,bkhe->bhqk", query, keys, preferred_element_type=jnp.float32
    ) * head_dim ** (-0.5)
    probs = jax.nn.softmax(scores, axis=-1).astype(jnp.bfloat16)
    mixed = jnp.einsum("bhqk,bkhe->bqhe", probs, values, preferred_element_type=jnp.float32).astype(
        jnp.bfloat16
    )
    mixed = mixed.reshape(row_count, quarter)
    attn_part = jnp.dot(mixed, collect(proj_weight, DP, 1), preferred_element_type=jnp.float32)
    attn = (
        lax.psum(attn_part.astype(jnp.bfloat16), "mp")
        .astype(jnp.float32)
        .reshape(image_count, tokens, width)
    )
    first_sum = images_f + gate_a[:, None] * attn
    hidden_two = (layer_norm(first_sum) * (1.0 + scale_m[:, None]) + shift_m[:, None]).astype(
        jnp.bfloat16
    )
    hidden_two = hidden_two.reshape(row_count, width)
    ff_quarter = fc1_weight.shape[1]
    columns = hidden_two
    up = jnp.dot(columns, gathered_by_axis(fc1_weight, DP, 0), preferred_element_type=jnp.float32)
    gelu_h = (
        jax.nn.gelu(up, approximate=True)
        .astype(jnp.bfloat16)
        .reshape(image_count, tokens, ff_quarter)
    )
    down_full = gathered_by_axis(fc2_weight, DP, 1)
    token_share = tokens // lax.axis_size("mp")
    mlp = sum_at_owner(
        jnp.einsum("btf,fd->tbd", gelu_h, down_full, preferred_element_type=jnp.float32).astype(
            jnp.bfloat16
        ),
        "mp",
        0,
    )
    token_start = lax.axis_index("mp") * token_share
    own_first = lax.dynamic_slice_in_dim(first_sum, token_start, token_share, 1).transpose(1, 0, 2)
    second_sum = own_first + gate_m[None] * mlp
    fin = (layer_norm(second_sum) * (1.0 + scale_f[None]) + shift_f[None]).astype(jnp.bfloat16)
    noise = jnp.einsum("tbd,do->bto", fin, out_weight, preferred_element_type=jnp.float32)
    noise = noise.reshape(2, pair_count, token_share * out_weight.shape[1])
    return noise[1] + guidance[0] * (noise[0] - noise[1])


def solution(mesh):
    torus = Mesh(
        mesh.devices.reshape(mesh.shape["group"], 8, 4, 2, mesh.shape["mp"]),
        ("group", "dp_0", "dp_1", "dp_2", "mp"),
    )
    placed = (
        P(GROUP_DP, None, None),
        P(GROUP_DP),
        P(GROUP_DP),
        P(GROUP_DP),
        P(),
        P(None, "mp"),
        P(None, "mp"),
        P("mp", DP),
        P("mp", None),
        P(None, DP, "mp"),
        P("mp", DP),
        P(DP, "mp"),
        P("mp", DP),
        P(),
    )
    return jax.shard_map(
        on_device, mesh=torus, in_specs=placed, out_specs=P(GROUP_DP, "mp"), check_vma=False
    )
```

profile of v0, /device:TPU:4, one launch (start us, length us, event | category | flops | bytes accessed | tf_op | source)
XLA Modules:
  0.0 341.8 jit_solution(6708045404015547400)
XLA Ops:
  7.4 1.6 copy.106
  10.3 1.0 constant_dynamic-slice_fusion
  11.3 0.1 copy.119
  11.4 1.0 constant_dynamic-slice_fusion.1
  12.4 0.1 copy.118
  12.5 0.1 copy.120
  12.7 0.6 copy-done.6
  13.2 0.7 broadcast_in_dim.50
  13.9 19.2 %all-to-all-start = ((bf16[64,2,288]{2,1,0:T(2,128)(2,1)}), bf16[64,2,288]{2,1,0:T(2,128)(2,1)S(1)}, u32[]{:S(2)}, u32[]{:S(2)}) async-start(bf16[64,2,288]{2,1,0:T(2,128)(2,1)} %broadcast_in_dim.50), calls=%async_computation | async-start | bytes 196608 | tf_op jit(solution)/shard_map/all_to_all | solution.py:15
  33.8 12.4 %all-to-all-done = bf16[64,2,288]{2,1,0:T(2,128)(2,1)S(1)} async-done(((bf16[64,2,288]{2,1,0:T(2,128)(2,1)}), bf16[64,2,288]{2,1,0:T(2,128)(2,1)S(1)}, u32[]{:S(2)}, u32[]{:S(2)}) %all-to-all-start) | async-done | bytes 73760 | tf_op jit(solution)/shard_map/all_to_all | solution.py:15
  46.3 1.1 convolution_convert_fusion.4
  47.4 0.7 broadcast_in_dim.84
  48.1 4.5 %all-to-all-start.1 = ((bf16[4,128,108]{1,2,0:T(8,128)(2,1)}), bf16[4,128,108]{1,2,0:T(8,128)(2,1)S(1)}, u32[]{:S(2)}, u32[]{:S(2)}) async-start(bf16[4,128,108]{1,2,0:T(8,128)(2,1)} %broadcast_in_dim.84), calls=%async_computation.1 | async-start | bytes 229376 | tf_op jit(solution)/shard_map/all_to_all | solution.py:15
  52.6 1.4 broadcast_select_fusion.1
  53.9 4.5 %all-to-all-done.1 = bf16[4,128,108]{1,2,0:T(8,128)(2,1)S(1)} async-done(((bf16[4,128,108]{1,2,0:T(8,128)(2,1)}), bf16[4,128,108]{1,2,0:T(8,128)(2,1)S(1)}, u32[]{:S(2)}, u32[]{:S(2)}) %all-to-all-start.1) | async-done | bytes 110624 | tf_op jit(solution)/shard_map/all_to_all | solution.py:15
  58.5 0.7 copy.104
  59.2 6.2 %all-to-all-start.2 = ((bf16[64,2,108]{2,1,0:T(2,128)(2,1)}), bf16[64,2,108]{2,1,0:T(2,128)(2,1)S(1)}, u32[]{:S(2)}, u32[]{:S(2)}) async-start(bf16[64,2,108]{2,1,0:T(2,128)(2,1)} %bitcast.7), calls=%async_computation.2 | async-start | bytes 65536 | tf_op jit(solution)/shard_map/all_to_all | solution.py:100
  65.3 0.2 convert_reduce_fusion
  65.6 12.4 %all-to-all-done.2 = bf16[64,2,108]{2,1,0:T(2,128)(2,1)S(1)} async-done(((bf16[64,2,108]{2,1,0:T(2,128)(2,1)}), bf16[64,2,108]{2,1,0:T(2,128)(2,1)S(1)}, u32[]{:S(2)}, u32[]{:S(2)}) %all-to-all-start.2) | async-done | bytes 27680 | tf_op jit(solution)/shard_map/all_to_all | solution.py:100
  78.0 1.1 broadcast_in_dim.85
  79.1 7.2 %all-to-all-start.3 = ((bf16[64,288,18]{1,2,0:T(8,128)(2,1)}), bf16[64,288,18]{1,2,0:T(8,128)(2,1)}, u32[]{:S(2)}, u32[]{:S(2)}) async-start(bf16[64,288,18]{1,2,0:T(8,128)(2,1)} %broadcast_in_dim.85), calls=%async_computation.3 | async-start | bytes 2359296 | tf_op jit(solution)/shard_map/all_to_all | solution.py:15
  86.4 0.4 fusion.20
  86.9 0.1 reshape.305
  87.1 1.7 fusion.16
  88.8 30.6 %all-to-all-done.3 = bf16[64,288,18]{1,2,0:T(8,128)(2,1)} async-done(((bf16[64,288,18]{1,2,0:T(8,128)(2,1)}), bf16[64,288,18]{1,2,0:T(8,128)(2,1)}, u32[]{:S(2)}, u32[]{:S(2)}) %all-to-all-start.3) | async-done | bytes 663584 | tf_op jit(solution)/shard_map/all_to_all | solution.py:15
  119.4 1.6 reshape.262
  121.0 51.8 %all-gather.8.cloned.1.call-done = bf16[3,1152,288]{2,0,1:T(4,128)(2,1)} async-done(((bf16[3,18,288]{2,0,1:T(4,128)(2,1)}), bf16[3,1152,288]{2,0,1:T(4,128)(2,1)}) %all-gather.8.cloned.1.call-update) | async-done | bytes 1990672 | tf_op jit(solution)/shard_map/all_gather | solution.py:117
  172.8 3.7 %fusion.26 = bf16[3,512,288]{1,2,0:T(8,128)(2,1)S(1)} fusion(bf16[3,1152,288]{2,0,1:T(4,128)(2,1)} %all-gather.8.cloned.1.call-done, bf16[512,1152]{1,0:T(8,128)(2,1)} %fusion.16), kind=kOutput, calls=%fused_computation.41 | convolution fusion | flops 1019658240 | bytes 4055040 | tf_op jit(solution)/shard_map/rd,kdc->krc/dot_general | solution.py:114
  176.6 0.9 fusion.62
  177.5 1.7 reshape_squeeze.10
  179.3 1.7 reshape_squeeze.11
  181.0 1.8 reshape_squeeze.9
  182.8 3.2 fusion.65
  186.0 2.0 fusion.30
  188.0 0.3 copy.112
  188.4 2.0 convolution_convert_fusion.2
  190.4 9.3 %all-gather = bf16[2,18,1152]{2,1,0:T(8,128)(2,1)S(1)} all-gather(bf16[1,18,1152]{2,1,0:T(8,128)(2,1)S(1)} %bitcast.125), channel_id=1, replica_groups=mesh['group'=2,'dp_0'=8,'dp_1'=4,'dp_2'=2,'mp'=4] {'dp_2'}, dimensions={0}, use_global_device_ids=true | all-gather | bytes 124416 | tf_op jit(solution)/shard_map/all_gather | solution.py:36
  199.8 11.3 %all-gather.1 = bf16[4,36,1152]{2,1,0:T(8,128)(2,1)S(1)} all-gather(bf16[1,36,1152]{2,1,0:T(8,128)(2,1)S(1)} %reshape.323), channel_id=1, replica_groups=mesh['group'=2,'dp_0'=8,'dp_1'=4,'dp_2'=2,'mp'=4] {'dp_1'}, dimensions={0}, use_global_device_ids=true | all-gather | bytes 414720 | tf_op jit(solution)/shard_map/all_gather | solution.py:36
  211.0 0.8 reshape.324
  211.9 10.3 %all-gather.2 = bf16[2,18,1152]{2,1,0:T(8,128)(2,1)S(1)} all-gather(bf16[1,18,1152]{2,1,0:T(8,128)(2,1)S(1)} %bitcast.126), channel_id=1, replica_groups=mesh['group'=2,'dp_0'=8,'dp_1'=4,'dp_2'=2,'mp'=4] {'dp_2'}, dimensions={0}, use_global_device_ids=true | all-gather | bytes 124416 | tf_op jit(solution)/shard_map/all_gather | solution.py:36
  222.2 12.4 %all-gather.3 = bf16[4,36,1152]{2,1,0:T(8,128)(2,1)S(1)} all-gather(bf16[1,36,1152]{2,1,0:T(8,128)(2,1)S(1)} %reshape.327), channel_id=1, replica_groups=mesh['group'=2,'dp_0'=8,'dp_1'=4,'dp_2'=2,'mp'=4] {'dp_1'}, dimensions={0}, use_global_device_ids=true | all-gather | bytes 414720 | tf_op jit(solution)/shard_map/all_gather | solution.py:36
  234.7 0.8 reshape.328
  235.6 0.3 convolution_convert_fusion
  235.9 0.6 broadcast_in_dim.86
  236.5 3.4 %all-to-all-start.5 = ((bf16[4,2,2304]{2,1,0:T(2,128)(2,1)}), bf16[4,2,2304]{2,1,0:T(2,128)(2,1)S(1)}, u32[]{:S(2)}, u32[]{:S(2)}) async-start(bf16[4,2,2304]{2,1,0:T(2,128)(2,1)} %broadcast_in_dim.86), calls=%async_computation.5 | async-start | bytes 73728 | tf_op jit(solution)/shard_map/all_to_all | solution.py:15
  240.0 21.1 %all-reduce.2.cloned.1.call-done = bf16[512,1152]{1,0:T(8,128)(2,1)} async-done(((bf16[512,1152]{1,0:T(8,128)(2,1)}), bf16[512,1152]{1,0:T(8,128)(2,1)}) %all-reduce.2.cloned.1.call-update) | async-done | bytes 1179664 | tf_op jit(solution)/shard_map/psum | solution.py:133
  261.1 1.7 fusion.60
  262.8 1.4 copy-done.1
  264.2 0.4 multiply_reduce_fusion
  264.6 0.3 copy-done.2
  264.9 2.0 fusion.12
  266.9 4.0 %fusion.11 = bf16[512,1152]{1,0:T(8,128)(2,1)S(1)} fusion(bf16[512,1152]{1,0:T(8,128)(2,1)} %fusion.12, bf16[1152,1152]{1,0:T(8,128)(2,1)} %all-gather.10.cloned.1.call-done), kind=kOutput, calls=%fused_computation.15 | convolution fusion | flops 1364262912 | bytes 5013504 | tf_op jit(solution)/shard_map/dot_general | solution.py:144
  271.0 25.5 %all-gather.12.cloned.1.call-done = bf16[1152,1152]{0,1:T(8,128)(2,1)} async-done(((bf16[1152,144]{0,1:T(8,128)(2,1)}), bf16[1152,1152]{0,1:T(8,128)(2,1)}) %all-gather.12.cloned.1.call-update) | async-done | bytes 2654224 | tf_op jit(solution)/shard_map/all_gather | solution.py:36
  296.4 3.6 %convolution_convert_fusion.1 = bf16[2,256,1152]{2,1,0:T(8,128)(2,1)S(1)} fusion(bf16[2,256,1152]{2,1,0:T(8,128)(2,1)S(1)} %bitcast.131, bf16[1152,1152]{0,1:T(8,128)(2,1)} %all-gather.12.cloned.1.call-done), kind=kOutput, calls=%fused_computation.3 | convolution fusion | flops 1359544320 | bytes 5013504 | tf_op jit(solution)/shard_map/btf,fd->tbd/dot_general | solution.py:153
  300.0 1.1 copy.113
  301.2 4.8 %all-to-all-start.4 = ((bf16[4,64,2,1152]{3,1,2,0:T(8,128)(2,1)}), bf16[4,64,2,1152]{3,1,2,0:T(8,128)(2,1)S(1)}, u32[]{:S(2)}, u32[]{:S(2)}) async-start(bf16[4,64,2,1152]{3,1,2,0:T(8,128)(2,1)} %copy.113), calls=%async_computation.4 | async-start | bytes 2359296 | tf_op jit(solution)/shard_map/all_to_all | solution.py:48
  306.7 24.8 %all-to-all-done.4 = bf16[4,64,2,1152]{3,1,2,0:T(8,128)(2,1)S(1)} async-done(((bf16[4,64,2,1152]{3,1,2,0:T(8,128)(2,1)}), bf16[4,64,2,1152]{3,1,2,0:T(8,128)(2,1)S(1)}, u32[]{:S(2)}, u32[]{:S(2)}) %all-to-all-start.4) | async-done | bytes 1179680 | tf_op jit(solution)/shard_map/all_to_all | solution.py:48
  331.5 0.2 convert_reduce_fusion.1
  331.6 1.2 fusion.59
  332.8 0.2 multiply_reduce_fusion.2
  333.1 0.3 convolution_bitcast_fusion
  333.4 0.1 copy.115
  333.5 0.1 squeeze.6
  333.8 0.6 multiply_add_fusion
  (51 shorter events, 0.8 us)
Async XLA Ops:
  7.4 228.2 %copy-start = (bf16[288,2304]{1,0:T(8,128)(2,1)S(1)}, bf16[288,2304]{1,0:T(8,128)(2,1)}, u32[]{:S(2)}) copy-start(bf16[288,2304]{1,0:T(8,128)(2,1)} %param.22) | copy-start | bytes 3981316
  7.4 165.5 %all-gather.8.cloned.1.call-start = ((), (), s32[]{:S(2)}) async-start(), calls=%async_computation.6 | async-start | bytes 3594240 | tf_op jit(solution)/shard_map/all_gather | solution.py:117
  12.7 0.6 copy-start.6
  13.9 64.1 %copy-start.5 = (bf16[288,18]{0,1:T(8,128)(2,1)S(1)}, bf16[288,18]{0,1:T(8,128)(2,1)}, u32[]{:S(2)}) copy-start(bf16[288,18]{0,1:T(8,128)(2,1)} %param.24) | copy-start | bytes 31108
  13.9 32.3 %all-to-all-start = ((bf16[64,2,288]{2,1,0:T(2,128)(2,1)}), bf16[64,2,288]{2,1,0:T(2,128)(2,1)S(1)}, u32[]{:S(2)}, u32[]{:S(2)}) async-start(bf16[64,2,288]{2,1,0:T(2,128)(2,1)} %broadcast_in_dim.50), calls=%async_computation | async-start | bytes 196608 | tf_op jit(solution)/shard_map/all_to_all | solution.py:15
  48.1 10.4 %all-to-all-start.1 = ((bf16[4,128,108]{1,2,0:T(8,128)(2,1)}), bf16[4,128,108]{1,2,0:T(8,128)(2,1)S(1)}, u32[]{:S(2)}, u32[]{:S(2)}) async-start(bf16[4,128,108]{1,2,0:T(8,128)(2,1)} %broadcast_in_dim.84), calls=%async_computation.1 | async-start | bytes 229376 | tf_op jit(solution)/shard_map/all_to_all | solution.py:15
  59.2 18.8 %all-to-all-start.2 = ((bf16[64,2,108]{2,1,0:T(2,128)(2,1)}), bf16[64,2,108]{2,1,0:T(2,128)(2,1)S(1)}, u32[]{:S(2)}, u32[]{:S(2)}) async-start(bf16[64,2,108]{2,1,0:T(2,128)(2,1)} %bitcast.7), calls=%async_computation.2 | async-start | bytes 65536 | tf_op jit(solution)/shard_map/all_to_all | solution.py:100
  79.1 40.3 %all-to-all-start.3 = ((bf16[64,288,18]{1,2,0:T(8,128)(2,1)}), bf16[64,288,18]{1,2,0:T(8,128)(2,1)}, u32[]{:S(2)}, u32[]{:S(2)}) async-start(bf16[64,288,18]{1,2,0:T(8,128)(2,1)} %broadcast_in_dim.85), calls=%async_computation.3 | async-start | bytes 2359296 | tf_op jit(solution)/shard_map/all_to_all | solution.py:15
  86.3 174.8 %all-reduce.2.cloned.1.call-start = ((), (), s32[]{:S(2)}) async-start(), calls=%async_computation.7 | async-start | bytes 2359296 | tf_op jit(solution)/shard_map/psum | solution.py:133
  188.0 2.4 copy-start.3
  188.4 23.6 %copy-start.4 = (bf16[1152,18]{0,1:T(8,128)(2,1)S(1)}, bf16[1152,18]{0,1:T(8,128)(2,1)}, u32[]{:S(2)}) copy-start(bf16[1152,18]{0,1:T(8,128)(2,1)} %param.26) | copy-start | bytes 124420
  190.3 45.2 %copy-start.7 = (bf16[2,288]{1,0:T(2,128)(2,1)S(1)}, bf16[2,288]{1,0:T(2,128)(2,1)}, u32[]{:S(2)}) copy-start(bf16[2,288]{1,0:T(2,128)(2,1)} %copy-done.6) | copy-start | bytes 3460
  190.4 76.6 %all-gather.10.cloned.1.call-start = ((), (), s32[]{:S(2)}) async-start(), calls=%async_computation.8 | async-start | bytes 2985984 | tf_op jit(solution)/shard_map/all_gather | solution.py:36
  211.9 84.6 %all-gather.12.cloned.1.call-start = ((), (), s32[]{:S(2)}) async-start(), calls=%async_computation.9 | async-start | bytes 2985984 | tf_op jit(solution)/shard_map/all_gather | solution.py:36
  236.5 64.7 %all-to-all-start.5 = ((bf16[4,2,2304]{2,1,0:T(2,128)(2,1)}), bf16[4,2,2304]{2,1,0:T(2,128)(2,1)S(1)}, u32[]{:S(2)}, u32[]{:S(2)}) async-start(bf16[4,2,2304]{2,1,0:T(2,128)(2,1)} %broadcast_in_dim.86), calls=%async_computation.5 | async-start | bytes 73728 | tf_op jit(solution)/shard_map/all_to_all | solution.py:15
  262.8 1.4 copy-start.1
  262.8 2.1 copy-start.2
  301.2 30.3 %all-to-all-start.4 = ((bf16[4,64,2,1152]{3,1,2,0:T(8,128)(2,1)}), bf16[4,64,2,1152]{3,1,2,0:T(8,128)(2,1)S(1)}, u32[]{:S(2)}, u32[]{:S(2)}) async-start(bf16[4,64,2,1152]{3,1,2,0:T(8,128)(2,1)} %copy.113), calls=%async_computation.4 | async-start | bytes 2359296 | tf_op jit(solution)/shard_map/all_to_all | solution.py:48
  305.9 27.1 %copy-start.8 = (bf16[1152,16]{0,1:T(8,128)(2,1)S(1)}, bf16[1152,16]{0,1:T(8,128)(2,1)}, u32[]{:S(2)}) copy-start(bf16[1152,16]{0,1:T(8,128)(2,1)} %param.27) | copy-start | bytes 110596
Sparse Core Ops, SparseCore 0:
  12.5 160.2 all-gather.7
  190.5 70.5 all-reduce.1
Sparse Core Ops, SparseCore 1:
  212.0 38.8 all-gather.9
  252.8 43.6 all-gather.11
where the time goes:
time: 343 us; the launch traced here: 342 us
  waiting for transfers between devices  183 us (53%)
  starting transfers between devices  45.4 us (13%)
  blocking collectives  43.3 us (13%)
  local copies, waits for them, and re-layouts  21.6 us (6%)
  matrix products  20.2 us (6%)
  between operations  17.8 us (5%)
  other arithmetic  10.3 us (3%)
    all_gather x1, waiting for transfers between devices, on_device(): lax.all_gather(qkv_weight, DP, axis=1, tiled=True)  51.8 us
    all_to_all x4, waiting for transfers between devices, from_everyone(): lax.all_to_all(jnp.broadcast_to(x[None], (size, *x.shape)), axis, 0, 0, t...  47.6 us
    all_gather x4, blocking collectives, gathered_by_axis(): x = lax.all_gather(x, axis, axis=dim, tiled=True)  43.3 us
    all_to_all x4, starting transfers between devices, from_everyone(): lax.all_to_all(jnp.broadcast_to(x[None], (size, *x.shape)), axis, 0, 0, t...  34.3 us
    all_gather x2, waiting for transfers between devices, gathered_by_axis(): x = lax.all_gather(x, axis, axis=dim, tiled=True)  25.5 us
    all_to_all x1, waiting for transfers between devices, sum_at_owner(): pieces = lax.all_to_all(cut_along(x, dim, size), axis, 0, 0, tiled=True)  24.8 us
    psum x1, waiting for transfers between devices, on_device(): lax.psum(attn_part.astype(jnp.bfloat16), 'mp').astype(jnp.float32)  21.1 us
    all_to_all x1, waiting for transfers between devices, on_device(): lax.all_to_all(summed.astype(jnp.bfloat16), DP, split_axis=0, concat_axis...  12.4 us
  transfers between devices with their start and end apart: 10, of which 8 were waited for; matrix products, arithmetic and copies ran while one was open for 8% of the time, Pallas kernels for 0%

commit v1 on v0

--- a/solution.py
+++ b/solution.py
@@ -8,6 +8,11 @@
 CLASSES = 1000
 DP = ("dp_0", "dp_1", "dp_2")
 GROUP_DP = ("group", "dp_0", "dp_1", "dp_2")
+
+
+def stack_and_merge(x, mesh_axis, dim):
+    tiles = lax.all_gather(x, mesh_axis)
+    return jnp.concatenate(tiles, axis=dim)
 
 
 def from_everyone(x, axis):
@@ -114,7 +119,7 @@
     qkv = jnp.einsum(
         "rd,kdc->krc",
         columns,
-        lax.all_gather(qkv_weight, DP, axis=1, tiled=True),
+        stack_and_merge(qkv_weight, DP, 1),
         preferred_element_type=jnp.float32,
     ).astype(jnp.bfloat16)
     query = qkv[0].reshape(image_count, tokens, local_heads, head_dim)

time: 343 us -> 358 us (1.044)
  local copies, waits for them, and re-layouts: 21.6 us -> 29.9 us
  waiting for transfers between devices: 183 us -> 191 us
    all_gather x1, waiting for transfers between devices: 51.8 us -> 58.3 us  [stack_and_merge(): tiles = lax.all_gather(x, mesh_axis)]
    reshape x0 -> x1, local copies, waits for them, and re-layouts: none -> 5.65 us  [stack_and_merge(): return jnp.concatenate(tiles, axis=dim)]
    all_gather x0 -> x1, local copies, waits for them, and re-layouts: none -> 4.16 us  [stack_and_merge(): tiles = lax.all_gather(x, mesh_axis)]
where the time goes in v1:
time: 358 us; the launch traced here: 357 us
  waiting for transfers between devices  191 us (53%)
  starting transfers between devices  45.4 us (13%)
  blocking collectives  43.3 us (12%)
  local copies, waits for them, and re-layouts  29.9 us (8%)
  matrix products  19.1 us (5%)
  between operations  17.8 us (5%)
  other arithmetic  10.1 us (3%)
    all_gather x1, waiting for transfers between devices, stack_and_merge(): tiles = lax.all_gather(x, mesh_axis)  58.3 us
    all_to_all x4, waiting for transfers between devices, from_everyone(): lax.all_to_all(jnp.broadcast_to(x[None], (size, *x.shape)), axis, 0, 0, t...  48.4 us
    all_gather x4, blocking collectives, gathered_by_axis(): x = lax.all_gather(x, axis, axis=dim, tiled=True)  43.3 us
    all_to_all x4, starting transfers between devices, from_everyone(): lax.all_to_all(jnp.broadcast_to(x[None], (size, *x.shape)), axis, 0, 0, t...  34.2 us
    all_gather x2, waiting for transfers between devices, gathered_by_axis(): x = lax.all_gather(x, axis, axis=dim, tiled=True)  25.6 us
    all_to_all x1, waiting for transfers between devices, sum_at_owner(): pieces = lax.all_to_all(cut_along(x, dim, size), axis, 0, 0, tiled=True)  24.8 us
    psum x1, waiting for transfers between devices, on_device(): lax.psum(attn_part.astype(jnp.bfloat16), 'mp').astype(jnp.float32)  21.1 us
    all_to_all x1, waiting for transfers between devices, on_device(): lax.all_to_all(summed.astype(jnp.bfloat16), DP, split_axis=0, concat_axis...  12.2 us
  transfers between devices with their start and end apart: 10, of which 8 were waited for; matrix products, arithmetic and copies ran while one was open for 8% of the time, Pallas kernels for 0%

profile of v1, /device:TPU:4, one launch (start us, length us, event | category | flops | bytes accessed | tf_op | source)
XLA Modules:
  0.0 356.7 jit_solution(16617043603877623151)
XLA Ops:
  7.4 0.7 all-gather.13.cloned.1.call-update
  9.4 1.1 constant_dynamic-slice_fusion
  10.6 1.0 constant_dynamic-slice_fusion.1
  11.7 0.1 copy.126
  11.9 0.6 copy-done.7
  12.4 0.7 broadcast_in_dim.50
  13.1 19.1 %all-to-all-start = ((bf16[64,2,288]{2,1,0:T(2,128)(2,1)}), bf16[64,2,288]{2,1,0:T(2,128)(2,1)S(1)}, u32[]{:S(2)}, u32[]{:S(2)}) async-start(bf16[64,2,288]{2,1,0:T(2,128)(2,1)} %broadcast_in_dim.50), calls=%async_computation | async-start | bytes 196608 | tf_op jit(solution)/shard_map/all_to_all | solution.py:20
  32.8 1.4 broadcast_select_fusion.1
  34.2 0.2 convert_reduce_fusion
  34.4 10.7 %all-to-all-done = bf16[64,2,288]{2,1,0:T(2,128)(2,1)S(1)} async-done(((bf16[64,2,288]{2,1,0:T(2,128)(2,1)}), bf16[64,2,288]{2,1,0:T(2,128)(2,1)S(1)}, u32[]{:S(2)}, u32[]{:S(2)}) %all-to-all-start) | async-done | bytes 73760 | tf_op jit(solution)/shard_map/all_to_all | solution.py:20
  45.3 0.2 convolution_convert_fusion.5
  45.5 0.7 broadcast_in_dim.84
  46.1 4.6 %all-to-all-start.1 = ((bf16[4,128,108]{1,2,0:T(8,128)(2,1)}), bf16[4,128,108]{1,2,0:T(8,128)(2,1)S(1)}, u32[]{:S(2)}, u32[]{:S(2)}) async-start(bf16[4,128,108]{1,2,0:T(8,128)(2,1)} %broadcast_in_dim.84), calls=%async_computation.1 | async-start | bytes 229376 | tf_op jit(solution)/shard_map/all_to_all | solution.py:20
  50.7 5.9 %all-to-all-done.1 = bf16[4,128,108]{1,2,0:T(8,128)(2,1)S(1)} async-done(((bf16[4,128,108]{1,2,0:T(8,128)(2,1)}), bf16[4,128,108]{1,2,0:T(8,128)(2,1)S(1)}, u32[]{:S(2)}, u32[]{:S(2)}) %all-to-all-start.1) | async-done | bytes 110624 | tf_op jit(solution)/shard_map/all_to_all | solution.py:20
  56.6 0.7 copy.109
  57.3 6.2 %all-to-all-start.2 = ((bf16[64,2,108]{2,1,0:T(2,128)(2,1)}), bf16[64,2,108]{2,1,0:T(2,128)(2,1)S(1)}, u32[]{:S(2)}, u32[]{:S(2)}) async-start(bf16[64,2,108]{2,1,0:T(2,128)(2,1)} %bitcast.7), calls=%async_computation.2 | async-start | bytes 65536 | tf_op jit(solution)/shard_map/all_to_all | solution.py:105
  63.5 0.5 fusion.16
  64.0 12.2 %all-to-all-done.2 = bf16[64,2,108]{2,1,0:T(2,128)(2,1)S(1)} async-done(((bf16[64,2,108]{2,1,0:T(2,128)(2,1)}), bf16[64,2,108]{2,1,0:T(2,128)(2,1)S(1)}, u32[]{:S(2)}, u32[]{:S(2)}) %all-to-all-start.2) | async-done | bytes 27680 | tf_op jit(solution)/shard_map/all_to_all | solution.py:105
  76.2 1.2 broadcast_in_dim.85
  77.3 7.2 %all-to-all-start.3 = ((bf16[64,288,18]{1,2,0:T(8,128)(2,1)}), bf16[64,288,18]{1,2,0:T(8,128)(2,1)}, u32[]{:S(2)}, u32[]{:S(2)}) async-start(bf16[64,288,18]{1,2,0:T(8,128)(2,1)} %broadcast_in_dim.85), calls=%async_computation.3 | async-start | bytes 2359296 | tf_op jit(solution)/shard_map/all_to_all | solution.py:20
  84.6 0.1 reshape.367
  84.8 1.5 fusion.19
  86.3 31.8 %all-to-all-done.3 = bf16[64,288,18]{1,2,0:T(8,128)(2,1)} async-done(((bf16[64,288,18]{1,2,0:T(8,128)(2,1)}), bf16[64,288,18]{1,2,0:T(8,128)(2,1)}, u32[]{:S(2)}, u32[]{:S(2)}) %all-to-all-start.3) | async-done | bytes 663584 | tf_op jit(solution)/shard_map/all_to_all | solution.py:20
  118.1 1.6 reshape.324
  119.8 58.3 %all-gather.13.cloned.1.call-done = bf16[192,18,288]{2,1,0:T(8,128)(2,1)} async-done(((bf16[3,18,288]{2,1,0:T(8,128)(2,1)}), bf16[192,18,288]{2,1,0:T(8,128)(2,1)}) %all-gather.13.cloned.1.call-update) | async-done | bytes 1990672 | tf_op jit(solution)/shard_map/all_gather | solution.py:14
  178.0 4.2 %copy.154 = bf16[64,3,18,288]{3,2,0,1:T(8,128)(2,1)} copy(bf16[64,3,18,288]{3,2,1,0:T(8,128)(2,1)} %bitcast.113) | data formatting | bytes 3981312 | tf_op jit(solution)/shard_map/all_gather | solution.py:14
  182.2 5.6 %reshape.322 = bf16[3,1152,288]{2,1,0:T(8,128)(2,1)} reshape(bf16[3,64,18,288]{3,2,1,0:T(8,128)(2,1)} %bitcast.111) | data formatting | bytes 3981312 | tf_op jit(solution)/shard_map/reshape | solution.py:15
  187.9 3.5 fusion.21
  191.4 0.9 fusion.52
  192.3 1.7 reshape_squeeze.10
  194.0 1.7 reshape_squeeze.11
  195.8 1.8 reshape_squeeze.9
  197.5 3.2 fusion.55
  200.8 2.0 fusion.22
  202.8 0.3 copy.117
  203.2 2.0 convolution_convert_fusion.2
  205.2 9.3 %all-gather.1 = bf16[2,18,1152]{2,1,0:T(8,128)(2,1)S(1)} all-gather(bf16[1,18,1152]{2,1,0:T(8,128)(2,1)S(1)} %bitcast.120), channel_id=1, replica_groups=mesh['group'=2,'dp_0'=8,'dp_1'=4,'dp_2'=2,'mp'=4] {'dp_2'}, dimensions={0}, use_global_device_ids=true | all-gather | bytes 124416 | tf_op jit(solution)/shard_map/all_gather | solution.py:41
  214.5 11.3 %all-gather.2 = bf16[4,36,1152]{2,1,0:T(8,128)(2,1)S(1)} all-gather(bf16[1,36,1152]{2,1,0:T(8,128)(2,1)S(1)} %reshape.386), channel_id=1, replica_groups=mesh['group'=2,'dp_0'=8,'dp_1'=4,'dp_2'=2,'mp'=4] {'dp_1'}, dimensions={0}, use_global_device_ids=true | all-gather | bytes 414720 | tf_op jit(solution)/shard_map/all_gather | solution.py:41
  225.8 0.8 reshape.387
  226.7 10.3 %all-gather.3 = bf16[2,18,1152]{2,1,0:T(8,128)(2,1)S(1)} all-gather(bf16[1,18,1152]{2,1,0:T(8,128)(2,1)S(1)} %bitcast.121), channel_id=1, replica_groups=mesh['group'=2,'dp_0'=8,'dp_1'=4,'dp_2'=2,'mp'=4] {'dp_2'}, dimensions={0}, use_global_device_ids=true | all-gather | bytes 124416 | tf_op jit(solution)/shard_map/all_gather | solution.py:41
  237.0 12.4 %all-gather.4 = bf16[4,36,1152]{2,1,0:T(8,128)(2,1)S(1)} all-gather(bf16[1,36,1152]{2,1,0:T(8,128)(2,1)S(1)} %reshape.390), channel_id=1, replica_groups=mesh['group'=2,'dp_0'=8,'dp_1'=4,'dp_2'=2,'mp'=4] {'dp_1'}, dimensions={0}, use_global_device_ids=true | all-gather | bytes 414720 | tf_op jit(solution)/shard_map/all_gather | solution.py:41
  249.5 0.8 reshape.391
  250.4 0.3 convolution_convert_fusion
  250.6 0.6 broadcast_in_dim.86
  251.3 3.4 all-to-all-start.5
  254.7 21.1 %all-reduce.2.cloned.1.call-done = bf16[512,1152]{1,0:T(8,128)(2,1)} async-done(((bf16[512,1152]{1,0:T(8,128)(2,1)}), bf16[512,1152]{1,0:T(8,128)(2,1)}) %all-reduce.2.cloned.1.call-update) | async-done | bytes 1179664 | tf_op jit(solution)/shard_map/psum | solution.py:138
  275.8 1.7 fusion.51
  277.6 1.4 copy-done.1
  279.0 0.4 multiply_reduce_fusion
  279.4 0.3 copy-done.2
  279.7 2.0 fusion.10
  281.7 4.0 %fusion.9 = bf16[512,1152]{1,0:T(8,128)(2,1)S(1)} fusion(bf16[512,1152]{1,0:T(8,128)(2,1)} %fusion.10, bf16[1152,1152]{1,0:T(8,128)(2,1)} %all-gather.9.cloned.1.call-done), kind=kOutput, calls=%fused_computation.14 | convolution fusion | flops 1364262912 | bytes 5013504 | tf_op jit(solution)/shard_map/dot_general | solution.py:149
  285.7 25.6 %all-gather.11.cloned.1.call-done = bf16[1152,1152]{0,1:T(8,128)(2,1)} async-done(((bf16[1152,144]{0,1:T(8,128)(2,1)}), bf16[1152,1152]{0,1:T(8,128)(2,1)}) %all-gather.11.cloned.1.call-update) | async-done | bytes 2654224 | tf_op jit(solution)/shard_map/all_gather | solution.py:41
  311.3 3.6 %convolution_convert_fusion.1 = bf16[2,256,1152]{2,1,0:T(8,128)(2,1)S(1)} fusion(bf16[2,256,1152]{2,1,0:T(8,128)(2,1)S(1)} %bitcast.124, bf16[1152,1152]{0,1:T(8,128)(2,1)} %all-gather.11.cloned.1.call-done), kind=kOutput, calls=%fused_computation.4 | convolution fusion | flops 1359544320 | bytes 5013504 | tf_op jit(solution)/shard_map/btf,fd->tbd/dot_general | solution.py:158
  314.9 1.1 copy.118
  316.0 4.8 %all-to-all-start.4 = ((bf16[4,64,2,1152]{3,1,2,0:T(8,128)(2,1)}), bf16[4,64,2,1152]{3,1,2,0:T(8,128)(2,1)S(1)}, u32[]{:S(2)}, u32[]{:S(2)}) async-start(bf16[4,64,2,1152]{3,1,2,0:T(8,128)(2,1)} %copy.118), calls=%async_computation.4 | async-start | bytes 2359296 | tf_op jit(solution)/shard_map/all_to_all | solution.py:53
  321.6 24.8 %all-to-all-done.4 = bf16[4,64,2,1152]{3,1,2,0:T(8,128)(2,1)S(1)} async-done(((bf16[4,64,2,1152]{3,1,2,0:T(8,128)(2,1)}), bf16[4,64,2,1152]{3,1,2,0:T(8,128)(2,1)S(1)}, u32[]{:S(2)}, u32[]{:S(2)}) %all-to-all-start.4) | async-done | bytes 1179680 | tf_op jit(solution)/shard_map/all_to_all | solution.py:53
  346.3 0.2 convert_reduce_fusion.1
  346.5 1.2 fusion.50
  347.7 0.2 multiply_reduce_fusion.2
  348.0 0.3 convolution_bitcast_fusion
  348.2 0.1 copy.120
  348.4 0.1 squeeze.6
  348.7 0.6 multiply_add_fusion
  (52 shorter events, 1.0 us)
Async XLA Ops:
  7.4 243.0 %copy-start = (bf16[288,2304]{1,0:T(8,128)(2,1)S(1)}, bf16[288,2304]{1,0:T(8,128)(2,1)}, u32[]{:S(2)}) copy-start(bf16[288,2304]{1,0:T(8,128)(2,1)} %param.22) | copy-start | bytes 3981316
  7.4 170.7 %all-gather.13.cloned.1.call-start = ((), (), s32[]{:S(2)}) async-start(), calls=%async_computation.9 | async-start | bytes 3594240 | tf_op jit(solution)/shard_map/all_gather | solution.py:14
  9.4 35.9 %copy-start.3 = (bf16[288,108]{1,0:T(8,128)(2,1)S(1)}, bf16[288,108]{1,0:T(8,128)(2,1)}, u32[]{:S(2)}) copy-start(bf16[288,108]{1,0:T(8,128)(2,1)} %param.21) | copy-start | bytes 186628
  11.8 0.6 copy-start.7
  13.1 32.1 %all-to-all-start = ((bf16[64,2,288]{2,1,0:T(2,128)(2,1)}), bf16[64,2,288]{2,1,0:T(2,128)(2,1)S(1)}, u32[]{:S(2)}, u32[]{:S(2)}) async-start(bf16[64,2,288]{2,1,0:T(2,128)(2,1)} %broadcast_in_dim.50), calls=%async_computation | async-start | bytes 196608 | tf_op jit(solution)/shard_map/all_to_all | solution.py:20
  32.8 43.3 %copy-start.6 = (bf16[288,18]{0,1:T(8,128)(2,1)S(1)}, bf16[288,18]{0,1:T(8,128)(2,1)}, u32[]{:S(2)}) copy-start(bf16[288,18]{0,1:T(8,128)(2,1)} %param.24) | copy-start | bytes 31108
  46.1 10.5 %all-to-all-start.1 = ((bf16[4,128,108]{1,2,0:T(8,128)(2,1)}), bf16[4,128,108]{1,2,0:T(8,128)(2,1)S(1)}, u32[]{:S(2)}, u32[]{:S(2)}) async-start(bf16[4,128,108]{1,2,0:T(8,128)(2,1)} %broadcast_in_dim.84), calls=%async_computation.1 | async-start | bytes 229376 | tf_op jit(solution)/shard_map/all_to_all | solution.py:20
  57.3 18.8 %all-to-all-start.2 = ((bf16[64,2,108]{2,1,0:T(2,128)(2,1)}), bf16[64,2,108]{2,1,0:T(2,128)(2,1)S(1)}, u32[]{:S(2)}, u32[]{:S(2)}) async-start(bf16[64,2,108]{2,1,0:T(2,128)(2,1)} %bitcast.7), calls=%async_computation.2 | async-start | bytes 65536 | tf_op jit(solution)/shard_map/all_to_all | solution.py:105
  77.3 40.8 %all-to-all-start.3 = ((bf16[64,288,18]{1,2,0:T(8,128)(2,1)}), bf16[64,288,18]{1,2,0:T(8,128)(2,1)}, u32[]{:S(2)}, u32[]{:S(2)}) async-start(bf16[64,288,18]{1,2,0:T(8,128)(2,1)} %broadcast_in_dim.85), calls=%async_computation.3 | async-start | bytes 2359296 | tf_op jit(solution)/shard_map/all_to_all | solution.py:20
  84.5 191.3 %all-reduce.2.cloned.1.call-start = ((), (), s32[]{:S(2)}) async-start(), calls=%async_computation.6 | async-start | bytes 2359296 | tf_op jit(solution)/shard_map/psum | solution.py:138
  202.8 2.4 copy-start.4
  203.1 23.6 %copy-start.5 = (bf16[1152,18]{0,1:T(8,128)(2,1)S(1)}, bf16[1152,18]{0,1:T(8,128)(2,1)}, u32[]{:S(2)}) copy-start(bf16[1152,18]{0,1:T(8,128)(2,1)} %param.26) | copy-start | bytes 124420
  205.1 45.2 %copy-start.8 = (bf16[2,288]{1,0:T(2,128)(2,1)S(1)}, bf16[2,288]{1,0:T(2,128)(2,1)}, u32[]{:S(2)}) copy-start(bf16[2,288]{1,0:T(2,128)(2,1)} %copy-done.7) | copy-start | bytes 3460
  205.1 76.6 %all-gather.9.cloned.1.call-start = ((), (), s32[]{:S(2)}) async-start(), calls=%async_computation.7 | async-start | bytes 2985984 | tf_op jit(solution)/shard_map/all_gather | solution.py:41
  226.6 84.7 %all-gather.11.cloned.1.call-start = ((), (), s32[]{:S(2)}) async-start(), calls=%async_computation.8 | async-start | bytes 2985984 | tf_op jit(solution)/shard_map/all_gather | solution.py:41
  251.3 64.7 %all-to-all-start.5 = ((bf16[4,2,2304]{2,1,0:T(2,128)(2,1)}), bf16[4,2,2304]{2,1,0:T(2,128)(2,1)S(1)}, u32[]{:S(2)}, u32[]{:S(2)}) async-start(bf16[4,2,2304]{2,1,0:T(2,128)(2,1)} %broadcast_in_dim.86), calls=%async_computation.5 | async-start | bytes 73728 | tf_op jit(solution)/shard_map/all_to_all | solution.py:20
  277.6 1.4 copy-start.1
  277.6 2.1 copy-start.2
  316.0 30.3 %all-to-all-start.4 = ((bf16[4,64,2,1152]{3,1,2,0:T(8,128)(2,1)}), bf16[4,64,2,1152]{3,1,2,0:T(8,128)(2,1)S(1)}, u32[]{:S(2)}, u32[]{:S(2)}) async-start(bf16[4,64,2,1152]{3,1,2,0:T(8,128)(2,1)} %copy.118), calls=%async_computation.4 | async-start | bytes 2359296 | tf_op jit(solution)/shard_map/all_to_all | solution.py:53
  320.8 27.1 %copy-start.9 = (bf16[1152,16]{0,1:T(8,128)(2,1)S(1)}, bf16[1152,16]{0,1:T(8,128)(2,1)}, u32[]{:S(2)}) copy-start(bf16[1152,16]{0,1:T(8,128)(2,1)} %param.27) | copy-start | bytes 110596
Sparse Core Ops, SparseCore 0:
  12.5 165.4 all-gather.12
  205.3 70.5 all-reduce.1
Sparse Core Ops, SparseCore 1:
  226.7 38.6 all-gather.8
  267.4 43.9 all-gather.10
